TPU v7x, 32 devices: a whole 2x2x4 slice. The times are simulated.
32 devices in a mesh: row: 8 (over y, x, core), col: 4 (over z).
Axes of the slice: x: 2, y: 2, z: 4, core: 2. Of those that a mesh axis runs over, the one named last changes fastest.
Arguments:
- jacobian: float32 [2, 4096, 256], P(None, ('row', 'col')), may hold values from -0.25 to 0.25
Outputs:
- normal_tiles: float32 [8, 2, 4, 512, 512], P('row', None, 'col')
All inputs are finite; a program needn't handle non-finite values.
Results may differ from a plain program's by a relative error of at most 0.0003.
Values sent between devices are 32-bit elements; how exact they have to be, the bound alone decides.
A program may use at most 64 MiB of HBM per device.

v0:
```python
import jax
import jax.numpy as jnp
from jax import lax
from jax.sharding import PartitionSpec as P


def from_partner(block, axis, distance):
    count = lax.axis_size(axis)
    route = []
    for low in range(count):
        high = low | 1 << distance
        if high != low and high < count:
            route += [(low, high), (high, low)]
    return lax.ppermute(block, axis, route)


def partner_rows(block, bit_number):
    return from_partner(block, ("row", "col"), bit_number)


def body(jacobian):
    row_index = lax.axis_index("row")
    col_index = lax.axis_index("col")
    col_count = lax.axis_size("col")
    cycles = lax.axis_size("row") // col_count
    panel_count = jacobian.shape[0]
    width = jacobian.shape[2]
    own_tile = lax.all_gather(jacobian, "col", axis=1, tiled=True)
    tile_size = own_tile.shape[1]
    col_bits = col_count.bit_length() - 1
    low_row = row_index % col_count
    moved = jacobian
    for bit_number in range(col_bits):
        first = partner_rows(moved, bit_number)
        second = partner_rows(first, bit_number + col_bits)
        differ = low_row >> bit_number & 1 != col_index >> bit_number & 1
        moved = jnp.where(differ, second, moved)
    gathered = lax.all_gather(moved, "row", axis=1, tiled=True)
    gathered = gathered.reshape(panel_count, cycles, tile_size, width)
    partners = [gathered[:, turn_index] for turn_index in range(cycles)]

    def product(partner):
        return jnp.einsum("pak,pbk->ab", own_tile, partner, precision=lax.Precision.HIGHEST)

    def empty_tile(partner):
        return jnp.zeros((tile_size, tile_size), jnp.float32)

    results = []
    for turn_index in range(cycles):
        column_tile = col_index + col_count * turn_index
        results.append(
            lax.cond(column_tile <= row_index, product, empty_tile, partners[turn_index])
        )
    blocks = jnp.stack(results, 0)
    return blocks[None, :, None]


def solution(mesh):
    in_specs = (P(None, ("row", "col"), None),)
    out_specs = P("row", None, "col", None, None)
    return jax.shard_map(body, mesh=mesh, in_specs=in_specs, out_specs=out_specs, check_vma=False)
```

profile of v0, /device:TPU:4, one launch (start us, length us, event | category | flops | bytes accessed | tf_op | source)
XLA Modules:
  0.0 115.7 jit_solution(6772489944896085306)
XLA Ops:
  6.5 0.0 all-gather.3.cloned.1.call-start
  6.5 1.6 %collective-permute-start = (f32[2,128,256]{2,1,0:T(8,128)}, f32[2,128,256]{2,1,0:T(8,128)S(1)}, u32[]{:S(2)}, u32[]{:S(2)}) collective-permute-start(f32[2,128,256]{2,1,0:T(8,128)} %param.5), channel_id=1, source_target_pairs={{0,1},{1,0},{2,3},{3,2},{4,5},{5,4},{6,7},{7,6},{8,9},{9,8},{10,11... | collective-permute-start | bytes 786440 | tf_op jit(solution)/shard_map/ppermute | solution.py:14
  8.1 6.7 %collective-permute-done = f32[2,128,256]{2,1,0:T(8,128)S(1)} collective-permute-done((f32[2,128,256]{2,1,0:T(8,128)}, f32[2,128,256]{2,1,0:T(8,128)S(1)}, u32[]{:S(2)}, u32[]{:S(2)}) %collective-permute-start) | collective-permute-done | bytes 262176 | tf_op jit(solution)/shard_map/ppermute | solution.py:14
  14.8 0.0 collective-permute-start.1
  14.8 1.5 %collective-permute-done.1 = f32[2,128,256]{2,1,0:T(8,128)S(1)} collective-permute-done((f32[2,128,256]{2,1,0:T(8,128)S(1)}, f32[2,128,256]{2,1,0:T(8,128)S(1)}, u32[]{:S(2)}, u32[]{:S(2)}) %collective-permute-start.1) | collective-permute-done | bytes 262176 | tf_op jit(solution)/shard_map/ppermute | solution.py:14
  16.3 1.0 broadcast_select_fusion
  17.3 2.7 %collective-permute-start.2 = (f32[2,128,256]{2,1,0:T(8,128)S(1)}, f32[2,128,256]{2,1,0:T(8,128)S(1)}, u32[]{:S(2)}, u32[]{:S(2)}) collective-permute-start(f32[2,128,256]{2,1,0:T(8,128)S(1)} %broadcast_select_fusion), channel_id=1, source_target_pairs={{0,2},{2,0},{1,3},{3,1},{4,6},{6,4},{5,7},{7,5},{8,10},{10,8},{9,1... | collective-permute-start | bytes 786440 | tf_op jit(solution)/shard_map/ppermute | solution.py:14
  20.0 11.3 %collective-permute-done.2 = f32[2,128,256]{2,1,0:T(8,128)S(1)} collective-permute-done((f32[2,128,256]{2,1,0:T(8,128)S(1)}, f32[2,128,256]{2,1,0:T(8,128)S(1)}, u32[]{:S(2)}, u32[]{:S(2)}) %collective-permute-start.2) | collective-permute-done | bytes 262176 | tf_op jit(solution)/shard_map/ppermute | solution.py:14
  31.3 1.5 %collective-permute-start.3 = (f32[2,128,256]{2,1,0:T(8,128)S(1)}, f32[2,128,256]{2,1,0:T(8,128)S(1)}, u32[]{:S(2)}, u32[]{:S(2)}) collective-permute-start(f32[2,128,256]{2,1,0:T(8,128)S(1)} %collective-permute-done.2), channel_id=1, source_target_pairs={{0,8},{8,0},{1,9},{9,1},{2,10},{10,2},{3,11},{11,3},{4,12},{12,4},... | collective-permute-start | bytes 786440 | tf_op jit(solution)/shard_map/ppermute | solution.py:14
  32.8 5.1 %collective-permute-done.3 = f32[2,128,256]{2,1,0:T(8,128)S(1)} collective-permute-done((f32[2,128,256]{2,1,0:T(8,128)S(1)}, f32[2,128,256]{2,1,0:T(8,128)S(1)}, u32[]{:S(2)}, u32[]{:S(2)}) %collective-permute-start.3) | collective-permute-done | bytes 262176 | tf_op jit(solution)/shard_map/ppermute | solution.py:14
  37.8 0.7 broadcast_select_fusion.1
  38.6 0.0 all-gather.3.cloned.1.call-update
  38.6 0.0 all-gather.5.cloned.1.call-start
  38.7 0.7 all-gather.5.cloned.1.call-update
  39.4 30.0 %all-gather.3.cloned.1.call-done = f32[2,1024,256]{2,1,0:T(8,128)} async-done(((f32[2,128,256]{2,1,0:T(8,128)}), f32[2,1024,256]{2,1,0:T(8,128)}) %all-gather.3.cloned.1.call-update) | async-done | bytes 2097168 | tf_op jit(solution)/shard_map/all_gather | solution.py:38
  69.3 1.7 %copy.2 = f32[2,2,512,256]{3,2,0,1:T(8,128)S(1)} copy(f32[2,2,512,256]{3,2,1,0:T(8,128)} %bitcast.17) | data formatting | bytes 4194304 | tf_op jit(solution)/shard_map/cond | solution.py:52
  71.1 27.9 %all-gather.5.cloned.1.call-done = f32[2,512,256]{2,1,0:T(8,128)} async-done(((f32[2,128,256]{2,1,0:T(8,128)}), f32[2,512,256]{2,1,0:T(8,128)}) %all-gather.5.cloned.1.call-update) | async-done | bytes 1048592 | tf_op jit(solution)/shard_map/all_gather | solution.py:28
  99.0 3.1 %conditional.3 = (f32[1,512,512]{2,1,0:T(8,128)S(1)}) conditional(s32[]{:T(128)} %convert_element_type.7, () %tuple.23, (f32[2,2,512,256]{3,2,0,1:T(8,128)S(1)}, f32[2,512,256]{2,1,0:T(8,128)}) %tuple.24), branch_computations={%region_2.3_spmd, %region_3.4_spmd} | conditional | flops 1610612736 | bytes 3145736 | solution.py:52
  99.0 3.1 %convolution_bitcast_fusion.1 = f32[1,512,512]{2,1,0:T(8,128)S(1)} fusion(f32[2,512,256]{2,1,0:T(8,128)} %get-tuple-element.27, f32[2,2,512,256]{3,2,0,1:T(8,128)S(1)} %get-tuple-element.28), kind=kOutput, calls=%fused_computation.3 | convolution fusion | flops 1610612736 | bytes 3145728 | tf_op jit(solution)/shard_map/cond/branch_1_fun/pak,pbk->ab/dot_general | solution.py:43
  102.1 4.1 %conditional.2 = (f32[1,512,512]{2,1,0:T(8,128)}) conditional(s32[]{:T(128)} %convert_element_type.6, () %tuple.21, (f32[2,2,512,256]{3,2,0,1:T(8,128)S(1)}, f32[2,512,256]{2,1,0:T(8,128)}) %tuple.24), branch_computations={%region_0.1_spmd, %region_1.2_spmd} | conditional | flops 1610612736 | bytes 3145736 | solution.py:52
  102.1 4.1 %convolution_bitcast_fusion = f32[1,512,512]{2,1,0:T(8,128)} fusion(f32[2,512,256]{2,1,0:T(8,128)} %get-tuple-element.25, f32[2,2,512,256]{3,2,0,1:T(8,128)S(1)} %get-tuple-element.26), kind=kOutput, calls=%fused_computation | convolution fusion | flops 1610612736 | bytes 3145728 | tf_op jit(solution)/shard_map/cond/branch_1_fun/pak,pbk->ab/dot_general | solution.py:43
  106.2 2.7 %maximum_bitcast_fusion = f32[1,2,1,512,512]{4,3,2,1,0:T(8,128)} fusion(f32[1,512,512]{2,1,0:T(8,128)S(1)} %get-tuple-element.34, f32[1,512,512]{2,1,0:T(8,128)} %get-tuple-element.33), kind=kLoop, calls=%fused_computation.6 | loop fusion | flops 524288 | bytes 4194304 | tf_op jit(solution)/shard_map/broadcast_in_dim | solution.py:55
Async XLA Ops:
  6.5 62.8 %all-gather.3.cloned.1.call-start = ((), (), s32[]{:S(2)}) async-start(), calls=%async_computation | async-start | bytes 2359296 | tf_op jit(solution)/shard_map/all_gather | solution.py:38
  6.5 8.3 %collective-permute-start = (f32[2,128,256]{2,1,0:T(8,128)}, f32[2,128,256]{2,1,0:T(8,128)S(1)}, u32[]{:S(2)}, u32[]{:S(2)}) collective-permute-start(f32[2,128,256]{2,1,0:T(8,128)} %param.5), channel_id=1, source_target_pairs={{0,1},{1,0},{2,3},{3,2},{4,5},{5,4},{6,7},{7,6},{8,9},{9,8},{10,11... | collective-permute-start | bytes 786440 | tf_op jit(solution)/shard_map/ppermute | solution.py:14
  14.8 1.5 %collective-permute-start.1 = (f32[2,128,256]{2,1,0:T(8,128)S(1)}, f32[2,128,256]{2,1,0:T(8,128)S(1)}, u32[]{:S(2)}, u32[]{:S(2)}) collective-permute-start(f32[2,128,256]{2,1,0:T(8,128)S(1)} %collective-permute-done), channel_id=1, source_target_pairs={{0,4},{4,0},{1,5},{5,1},{2,6},{6,2},{3,7},{7,3},{8,12},{12,8},{9,1... | collective-permute-start | bytes 786440 | tf_op jit(solution)/shard_map/ppermute | solution.py:14
  17.3 14.0 %collective-permute-start.2 = (f32[2,128,256]{2,1,0:T(8,128)S(1)}, f32[2,128,256]{2,1,0:T(8,128)S(1)}, u32[]{:S(2)}, u32[]{:S(2)}) collective-permute-start(f32[2,128,256]{2,1,0:T(8,128)S(1)} %broadcast_select_fusion), channel_id=1, source_target_pairs={{0,2},{2,0},{1,3},{3,1},{4,6},{6,4},{5,7},{7,5},{8,10},{10,8},{9,1... | collective-permute-start | bytes 786440 | tf_op jit(solution)/shard_map/ppermute | solution.py:14
  31.3 6.5 %collective-permute-start.3 = (f32[2,128,256]{2,1,0:T(8,128)S(1)}, f32[2,128,256]{2,1,0:T(8,128)S(1)}, u32[]{:S(2)}, u32[]{:S(2)}) collective-permute-start(f32[2,128,256]{2,1,0:T(8,128)S(1)} %collective-permute-done.2), channel_id=1, source_target_pairs={{0,8},{8,0},{1,9},{9,1},{2,10},{10,2},{3,11},{11,3},{4,12},{12,4},... | collective-permute-start | bytes 786440 | tf_op jit(solution)/shard_map/ppermute | solution.py:14
  38.6 60.4 %all-gather.5.cloned.1.call-start = ((), (), s32[]{:S(2)}) async-start(), calls=%async_computation.1 | async-start | bytes 1310720 | tf_op jit(solution)/shard_map/all_gather | solution.py:28
Sparse Core Ops, SparseCore 0:
  38.7 30.5 all-gather.2
  70.9 28.0 all-gather.4
where the time goes:
time: 116 us
  waiting for transfers between devices  83.2 us (72%)
  between operations  13.4 us (12%)
  matrix products  7.14 us (6%)
  starting transfers between devices  5.77 us (5%)
  other arithmetic  4.43 us (4%)
  local copies, waits for them, and re-layouts  1.73 us (1%)
    all_gather x1, waiting for transfers between devices, body(): gathered = lax.all_gather(moved, 'row', axis=1, tiled=True)  30 us
    all_gather x1, waiting for transfers between devices, body(): own_tile = lax.all_gather(jacobian, 'col', axis=1, tiled=True)  27.9 us
    ppermute x4, waiting for transfers between devices, from_partner(): return lax.ppermute(block, axis, route)  24.6 us
    dot_general x2, matrix products, product(): jnp.einsum('pak,pbk->ab', own_tile, partner, precision=lax.Precision.HIGH...  7.14 us
    ppermute x4, starting transfers between devices, from_partner(): return lax.ppermute(block, axis, route)  5.72 us
    broadcast_in_dim x1, other arithmetic, body(): return blocks[None, :, None]  2.71 us
  transfers between devices with their start and end apart: 6, of which 6 were waited for; matrix products, arithmetic and copies ran while one was open for 1% of the time, Pallas kernels for 0%

commit v1 on v0

--- a/solution.py
+++ b/solution.py
@@ -2,6 +2,21 @@
 import jax.numpy as jnp
 from jax import lax
 from jax.sharding import PartitionSpec as P
+
+
+def core_convert(chunk):
+    axis_total = lax.axis_size("col")
+    crops = [chunk]
+    it = 0
+    while it < axis_total - 1:
+        state_next = lax.ppermute(
+            crops[-1], "col", [(h, (h + 1) % axis_total) for h in range(axis_total)]
+        )
+        crops.append(state_next)
+        it = it + 1
+    passed = jnp.concatenate(crops[::-1], 1)
+    known = jnp.roll(passed, (lax.axis_index("col") + 1) * chunk.shape[1], 1)
+    return known
 
 
 def from_partner(block, axis, distance):
@@ -25,7 +40,7 @@
     cycles = lax.axis_size("row") // col_count
     panel_count = jacobian.shape[0]
     width = jacobian.shape[2]
-    own_tile = lax.all_gather(jacobian, "col", axis=1, tiled=True)
+    own_tile = core_convert(jacobian)
     tile_size = own_tile.shape[1]
     col_bits = col_count.bit_length() - 1
     low_row = row_index % col_count

time: 116 us -> 102 us (0.88)
  waiting for transfers between devices: 83.2 us -> 71.6 us
  matrix products: 7.14 us -> 5.7 us
  starting transfers between devices: 5.77 us -> 4.37 us
  local copies, waits for them, and re-layouts: 1.73 us -> 2.89 us
    all_gather x1 -> x0, waiting for transfers between devices: 27.9 us -> none  [body(): own_tile = lax.all_gather(jacobian, 'col', axis=1, tiled=True)]
    ppermute x0 -> x3, waiting for transfers between devices: none -> 25.3 us  [core_convert(): lax.ppermute(crops[-1], 'col', [(h, (h + 1) % axis_total) for h in range(...]
    ppermute x4, waiting for transfers between devices: 24.6 us -> 20.3 us  [from_partner(): return lax.ppermute(block, axis, route)]
    all_gather x1, waiting for transfers between devices: 30 us -> 25.9 us  [body(): gathered = lax.all_gather(moved, 'row', axis=1, tiled=True)]
    ppermute x4, starting transfers between devices: 5.72 us -> 2.79 us  [from_partner(): return lax.ppermute(block, axis, route)]
    ppermute x0 -> x3, starting transfers between devices: none -> 1.58 us  [core_convert(): lax.ppermute(crops[-1], 'col', [(h, (h + 1) % axis_total) for h in range(...]
    dot_general x2, matrix products: 7.14 us -> 5.7 us  [product(): jnp.einsum('pak,pbk->ab', own_tile, partner, precision=lax.Precision.HIGH...]
  transfers between devices with their start and end apart: 6 -> 8, of which waited for: 6 -> 7; matrix products, arithmetic and copies ran while one was open for 1% -> 1% of each run, Pallas kernels for 0% -> 0%
where the time goes in v1:
time: 102 us
  waiting for transfers between devices  71.6 us (70%)
  between operations  13.5 us (13%)
  matrix products  5.7 us (6%)
  starting transfers between devices  4.37 us (4%)
  other arithmetic  3.81 us (4%)
  local copies, waits for them, and re-layouts  2.89 us (3%)
    all_gather x1, waiting for transfers between devices, body(): gathered = lax.all_gather(moved, 'row', axis=1, tiled=True)  25.9 us
    ppermute x3, waiting for transfers between devices, core_convert(): lax.ppermute(crops[-1], 'col', [(h, (h + 1) % axis_total) for h in range(...  25.3 us
    ppermute x4, waiting for transfers between devices, from_partner(): return lax.ppermute(block, axis, route)  20.3 us
    dot_general x2, matrix products, product(): jnp.einsum('pak,pbk->ab', own_tile, partner, precision=lax.Precision.HIGH...  5.7 us
    broadcast_in_dim x1, other arithmetic, body(): return blocks[None, :, None]  3.03 us
    ppermute x4, starting transfers between devices, from_partner(): return lax.ppermute(block, axis, route)  2.79 us
  transfers between devices with their start and end apart: 8, of which 7 were waited for; matrix products, arithmetic and copies ran while one was open for 1% of the time, Pallas kernels for 0%

profile of v1, /device:TPU:4, one launch (start us, length us, event | category | flops | bytes accessed | tf_op | source)
XLA Modules:
  0.0 101.9 jit_solution(9827314079498389836)
XLA Ops:
  6.5 0.0 copy-start
  6.5 0.0 all-gather.2.cloned.1.call-start
  6.5 1.6 %collective-permute-start.4 = (f32[2,128,256]{2,1,0:T(8,128)}, f32[2,128,256]{2,1,0:T(8,128)S(1)}, u32[]{:S(2)}, u32[]{:S(2)}) collective-permute-start(f32[2,128,256]{2,1,0:T(8,128)} %param.5), channel_id=1, source_target_pairs={{0,1},{1,2},{2,3},{3,0},{4,5},{5,6},{6,7},{7,4},{8,9},{9,10},{10,1... | collective-permute-start | bytes 786440 | tf_op jit(solution)/shard_map/ppermute | solution.py:12
  8.1 8.6 %collective-permute-done.4 = f32[2,128,256]{2,1,0:T(8,128)S(1)} collective-permute-done((f32[2,128,256]{2,1,0:T(8,128)}, f32[2,128,256]{2,1,0:T(8,128)S(1)}, u32[]{:S(2)}, u32[]{:S(2)}) %collective-permute-start.4) | collective-permute-done | bytes 262176 | tf_op jit(solution)/shard_map/ppermute | solution.py:12
  16.7 0.0 collective-permute-start.5
  16.7 1.2 %collective-permute-start = (f32[2,128,256]{2,1,0:T(8,128)}, f32[2,128,256]{2,1,0:T(8,128)S(1)}, u32[]{:S(2)}, u32[]{:S(2)}) collective-permute-start(f32[2,128,256]{2,1,0:T(8,128)} %param.5), channel_id=1, source_target_pairs={{0,1},{1,0},{2,3},{3,2},{4,5},{5,4},{6,7},{7,6},{8,9},{9,8},{10,11... | collective-permute-start | bytes 786440 | tf_op jit(solution)/shard_map/ppermute | solution.py:29
  17.9 9.7 %collective-permute-done.5 = f32[2,128,256]{2,1,0:T(8,128)S(1)} collective-permute-done((f32[2,128,256]{2,1,0:T(8,128)S(1)}, f32[2,128,256]{2,1,0:T(8,128)S(1)}, u32[]{:S(2)}, u32[]{:S(2)}) %collective-permute-start.5) | collective-permute-done | bytes 262176 | tf_op jit(solution)/shard_map/ppermute | solution.py:12
  27.7 0.0 collective-permute-start.6
  27.7 2.4 %collective-permute-done = f32[2,128,256]{2,1,0:T(8,128)S(1)} collective-permute-done((f32[2,128,256]{2,1,0:T(8,128)}, f32[2,128,256]{2,1,0:T(8,128)S(1)}, u32[]{:S(2)}, u32[]{:S(2)}) %collective-permute-start) | collective-permute-done | bytes 262176 | tf_op jit(solution)/shard_map/ppermute | solution.py:29
  30.1 0.0 collective-permute-start.1
  30.1 6.9 %collective-permute-done.6 = f32[2,128,256]{2,1,0:T(8,128)S(1)} collective-permute-done((f32[2,128,256]{2,1,0:T(8,128)S(1)}, f32[2,128,256]{2,1,0:T(8,128)S(1)}, u32[]{:S(2)}, u32[]{:S(2)}) %collective-permute-start.6) | collective-permute-done | bytes 262176 | tf_op jit(solution)/shard_map/ppermute | solution.py:12
  37.2 1.0 constant_dynamic-update-slice_fusion.4
  38.2 0.0 collective-permute-done.1
  38.2 0.0 copy-done
  38.3 0.1 collective-permute-start.2
  38.4 11.2 %collective-permute-done.2 = f32[2,128,256]{2,1,0:T(8,128)S(1)} collective-permute-done((f32[2,128,256]{2,1,0:T(8,128)S(1)}, f32[2,128,256]{2,1,0:T(8,128)S(1)}, u32[]{:S(2)}, u32[]{:S(2)}) %collective-permute-start.2) | collective-permute-done | bytes 262176 | tf_op jit(solution)/shard_map/ppermute | solution.py:29
  49.5 1.5 %collective-permute-start.3 = (f32[2,128,256]{2,1,0:T(8,128)S(1)}, f32[2,128,256]{2,1,0:T(8,128)S(1)}, u32[]{:S(2)}, u32[]{:S(2)}) collective-permute-start(f32[2,128,256]{2,1,0:T(8,128)S(1)} %collective-permute-done.2), channel_id=1, source_target_pairs={{0,8},{8,0},{1,9},{9,1},{2,10},{10,2},{3,11},{11,3},{4,12},{12,4},... | collective-permute-start | bytes 786440 | tf_op jit(solution)/shard_map/ppermute | solution.py:29
  51.0 6.7 %collective-permute-done.3 = f32[2,128,256]{2,1,0:T(8,128)S(1)} collective-permute-done((f32[2,128,256]{2,1,0:T(8,128)S(1)}, f32[2,128,256]{2,1,0:T(8,128)S(1)}, u32[]{:S(2)}, u32[]{:S(2)}) %collective-permute-start.3) | collective-permute-done | bytes 262176 | tf_op jit(solution)/shard_map/ppermute | solution.py:29
  57.8 0.7 broadcast_select_fusion.1
  58.5 0.0 all-gather.2.cloned.1.call-update
  58.5 0.1 constant_dynamic-slice_fusion
  58.6 25.9 %all-gather.2.cloned.1.call-done = f32[2,1024,256]{2,1,0:T(8,128)} async-done(((f32[2,128,256]{2,1,0:T(8,128)}), f32[2,1024,256]{2,1,0:T(8,128)}) %all-gather.2.cloned.1.call-update) | async-done | bytes 2097168 | tf_op jit(solution)/shard_map/all_gather | solution.py:53
  84.5 1.7 %copy.2 = f32[2,2,512,256]{3,2,0,1:T(8,128)S(1)} copy(f32[2,2,512,256]{3,2,1,0:T(8,128)} %bitcast.17) | data formatting | bytes 4194304 | tf_op jit(solution)/shard_map/cond | solution.py:67
  86.3 2.9 %conditional.3 = (f32[1,512,512]{2,1,0:T(8,128)}) conditional(s32[]{:T(128)} %convert_element_type.7, () %tuple.23, (f32[2,2,512,256]{3,2,0,1:T(8,128)S(1)}, f32[2,512,256]{2,1,0:T(8,128)S(1)}) %tuple.24), branch_computations={%region_2.3_spmd, %region_3.4_spmd} | conditional | flops 1610612736 | bytes 3145736 | solution.py:67
  86.3 2.9 %convolution_bitcast_fusion.1 = f32[1,512,512]{2,1,0:T(8,128)} fusion(f32[2,512,256]{2,1,0:T(8,128)S(1)} %get-tuple-element.27, f32[2,2,512,256]{3,2,0,1:T(8,128)S(1)} %get-tuple-element.28), kind=kOutput, calls=%fused_computation.3 | convolution fusion | flops 1610612736 | bytes 3145728 | tf_op jit(solution)/shard_map/cond/branch_1_fun/pak,pbk->ab/dot_general | solution.py:58
  89.2 2.8 %conditional.2 = (f32[1,512,512]{2,1,0:T(8,128)}) conditional(s32[]{:T(128)} %convert_element_type.6, () %tuple.21, (f32[2,2,512,256]{3,2,0,1:T(8,128)S(1)}, f32[2,512,256]{2,1,0:T(8,128)S(1)}) %tuple.24), branch_computations={%region_0.1_spmd, %region_1.2_spmd} | conditional | flops 1610612736 | bytes 3145736 | solution.py:67
  89.2 2.8 %convolution_bitcast_fusion = f32[1,512,512]{2,1,0:T(8,128)} fusion(f32[2,512,256]{2,1,0:T(8,128)S(1)} %get-tuple-element.25, f32[2,2,512,256]{3,2,0,1:T(8,128)S(1)} %get-tuple-element.26), kind=kOutput, calls=%fused_computation | convolution fusion | flops 1610612736 | bytes 3145728 | tf_op jit(solution)/shard_map/cond/branch_1_fun/pak,pbk->ab/dot_general | solution.py:58
  92.0 3.0 %maximum_bitcast_fusion = f32[1,2,1,512,512]{4,3,2,1,0:T(8,128)} fusion(f32[1,512,512]{2,1,0:T(8,128)} %get-tuple-element.36, f32[1,512,512]{2,1,0:T(8,128)} %get-tuple-element.35), kind=kLoop, calls=%fused_computation.6 | loop fusion | flops 524288 | bytes 4194304 | tf_op jit(solution)/shard_map/broadcast_in_dim | solution.py:70
  (7 shorter events, 0.2 us)
Async XLA Ops:
  6.5 31.7 %copy-start = (f32[2,128,256]{2,1,0:T(8,128)S(1)}, f32[2,128,256]{2,1,0:T(8,128)}, u32[]{:S(2)}) copy-start(f32[2,128,256]{2,1,0:T(8,128)} %param.5) | copy-start | bytes 786436
  6.5 78.0 %all-gather.2.cloned.1.call-start = ((), (), s32[]{:S(2)}) async-start(), calls=%async_computation | async-start | bytes 2359296 | tf_op jit(solution)/shard_map/all_gather | solution.py:53
  6.5 10.2 %collective-permute-start.4 = (f32[2,128,256]{2,1,0:T(8,128)}, f32[2,128,256]{2,1,0:T(8,128)S(1)}, u32[]{:S(2)}, u32[]{:S(2)}) collective-permute-start(f32[2,128,256]{2,1,0:T(8,128)} %param.5), channel_id=1, source_target_pairs={{0,1},{1,2},{2,3},{3,0},{4,5},{5,6},{6,7},{7,4},{8,9},{9,10},{10,1... | collective-permute-start | bytes 786440 | tf_op jit(solution)/shard_map/ppermute | solution.py:12
  16.7 11.0 %collective-permute-start.5 = (f32[2,128,256]{2,1,0:T(8,128)S(1)}, f32[2,128,256]{2,1,0:T(8,128)S(1)}, u32[]{:S(2)}, u32[]{:S(2)}) collective-permute-start(f32[2,128,256]{2,1,0:T(8,128)S(1)} %collective-permute-done.4), channel_id=1, source_target_pairs={{0,1},{1,2},{2,3},{3,0},{4,5},{5,6},{6,7},{7,4},{8,9},{9,10},{10,1... | collective-permute-start | bytes 786440 | tf_op jit(solution)/shard_map/ppermute | solution.py:12
  16.7 13.4 %collective-permute-start = (f32[2,128,256]{2,1,0:T(8,128)}, f32[2,128,256]{2,1,0:T(8,128)S(1)}, u32[]{:S(2)}, u32[]{:S(2)}) collective-permute-start(f32[2,128,256]{2,1,0:T(8,128)} %param.5), channel_id=1, source_target_pairs={{0,1},{1,0},{2,3},{3,2},{4,5},{5,4},{6,7},{7,6},{8,9},{9,8},{10,11... | collective-permute-start | bytes 786440 | tf_op jit(solution)/shard_map/ppermute | solution.py:29
  27.7 9.4 %collective-permute-start.6 = (f32[2,128,256]{2,1,0:T(8,128)S(1)}, f32[2,128,256]{2,1,0:T(8,128)S(1)}, u32[]{:S(2)}, u32[]{:S(2)}) collective-permute-start(f32[2,128,256]{2,1,0:T(8,128)S(1)} %collective-permute-done.5), channel_id=1, source_target_pairs={{0,1},{1,2},{2,3},{3,0},{4,5},{5,6},{6,7},{7,4},{8,9},{9,10},{10,1... | collective-permute-start | bytes 786440 | tf_op jit(solution)/shard_map/ppermute | solution.py:12
  30.1 8.1 %collective-permute-start.1 = (f32[2,128,256]{2,1,0:T(8,128)S(1)}, f32[2,128,256]{2,1,0:T(8,128)S(1)}, u32[]{:S(2)}, u32[]{:S(2)}) collective-permute-start(f32[2,128,256]{2,1,0:T(8,128)S(1)} %collective-permute-done), channel_id=1, source_target_pairs={{0,4},{4,0},{1,5},{5,1},{2,6},{6,2},{3,7},{7,3},{8,12},{12,8},{9,1... | collective-permute-start | bytes 786440 | tf_op jit(solution)/shard_map/ppermute | solution.py:29
  38.3 11.2 %collective-permute-start.2 = (f32[2,128,256]{2,1,0:T(8,128)S(1)}, f32[2,128,256]{2,1,0:T(8,128)S(1)}, u32[]{:S(2)}, u32[]{:S(2)}) collective-permute-start(f32[2,128,256]{2,1,0:T(8,128)S(1)} %get-tuple-element.34), channel_id=1, source_target_pairs={{0,2},{2,0},{1,3},{3,1},{4,6},{6,4},{5,7},{7,5},{8,10},{10,8},{9,1... | collective-permute-start | bytes 786440 | tf_op jit(solution)/shard_map/ppermute | solution.py:29
  49.5 8.2 %collective-permute-start.3 = (f32[2,128,256]{2,1,0:T(8,128)S(1)}, f32[2,128,256]{2,1,0:T(8,128)S(1)}, u32[]{:S(2)}, u32[]{:S(2)}) collective-permute-start(f32[2,128,256]{2,1,0:T(8,128)S(1)} %collective-permute-done.2), channel_id=1, source_target_pairs={{0,8},{8,0},{1,9},{9,1},{2,10},{10,2},{3,11},{11,3},{4,12},{12,4},... | collective-permute-start | bytes 786440 | tf_op jit(solution)/shard_map/ppermute | solution.py:29
Sparse Core Ops, SparseCore 0:
  58.6 25.8 all-gather.1
